TPU v7x, 512 devices: a 8x2x16 block of a 8x8x16 slice. The times are simulated.
512 devices in a mesh: grp: 2 (over y), tp: 128 (over x, z), sub: 2 (over core).
Axes of the slice: x: 8, y: 2, z: 16, core: 2. Of those that a mesh axis runs over, the one named last changes fastest.
The devices are a block of a 8x8x16 slice.
Arguments:
- hidden_in: bfloat16 [32, 2, 4096], P('grp', 'sub', 'tp'), parts along dimension 0, may hold values from -16 to 16
- norm_attn: float32 [8192], replicated, may hold values from 0.25 to 1.75
- w_query: bfloat16 [8192, 2, 4096], P(None, 'sub', 'tp'), may hold values from -0.0625 to 0.0625
- w_key: bfloat16 [8192, 2, 512], P(None, 'sub', 'tp'), may hold values from -0.0625 to 0.0625
- w_value: bfloat16 [8192, 2, 512], P(None, 'sub', 'tp'), may hold values from -0.0625 to 0.0625
- w_out: bfloat16 [2, 4096, 2, 4096], P('sub', None, None, 'tp'), may hold values from -0.0625 to 0.0625
- norm_ffn: float32 [8192], replicated, may hold values from 0.25 to 1.75
- w_gate: bfloat16 [2, 4096, 14336], P('sub', None, 'tp'), may hold values from -0.0625 to 0.0625
- w_up: bfloat16 [2, 4096, 14336], P('sub', None, 'tp'), may hold values from -0.0625 to 0.0625
- w_down: bfloat16 [14336, 2, 4096], P('tp', 'sub'), may hold values from -0.1875 to 0.1875
- cache_keys: bfloat16 [32, 1024, 8, 128], P('grp', 'tp', 'sub'), parts along dimension 0, may hold values from -250 to 250
- cache_values: bfloat16 [32, 1024, 8, 128], P('grp', 'tp', 'sub'), parts along dimension 0, may hold values from -6 to 6
- lengths: int32 [32], P('grp'), parts along dimension 0, may hold values from 1 to 1024, as said below
Outputs:
- hidden_out: bfloat16 [32, 2, 4096], P('grp', 'sub', 'tp'), parts along dimension 0
There are 2 independent parts, one for each index of `grp`. A program takes and returns all parts, laid end to end along the dimension named above; an argument that names none is the same for every part. Nothing has to cross between parts.
Inputs may be any that keep to these rules, and one draw needn't show every extreme that they name: `lengths`: some sequence has 1024 live positions and some has 1.
All inputs are finite; a program needn't handle non-finite values.
Results may differ from a plain program's by a relative error of at most 0.012.
The roundings to bfloat16 on the way count: a program that leaves them out, or rounds other values in their place, can miss the bound.
Values may be sent and summed in bfloat16 or wider, within the bound.
A program may use at most 128 MiB of HBM per device.

v0:
```python
import math
import jax
import jax.numpy as jnp
from jax import lax
from jax.sharding import Mesh
from jax.sharding import PartitionSpec as P

HD = 128
TP = ("tp_0", "tp_1")
epsilon = 1e-05
rope_base = 500000.0
floor_score = -1e30


def joined_along(parts, dim):
    shape = list(parts.shape[1:])
    shape[dim] *= parts.shape[0]
    return jnp.moveaxis(parts, 0, dim).reshape(shape)


def gather_in_order(array, axes, sequence):
    parts = array[None]
    for k in sequence:
        parts = lax.all_gather(parts, axes[k], axis=0, tiled=True)
    carried = [lax.axis_size(axes[k]) for k in reversed(sequence)]
    parts = parts.reshape(*carried, *array.shape)
    turned = sorted(range(len(sequence)), key=lambda place: sequence[len(sequence) - 1 - place])
    return parts.transpose(*turned, *range(len(sequence), parts.ndim)).reshape(-1, *array.shape)


def whole_of(array, axes, sequence, dim):
    return joined_along(gather_in_order(array, axes, sequence), dim)


def sent_to_all(array, axis):
    copies = jnp.broadcast_to(array, (lax.axis_size(axis), *array.shape))
    return lax.all_to_all(copies, axis, split_axis=0, concat_axis=0, tiled=True)


def gathered_copies(array, axis, dim):
    parts = sent_to_all(array, axis)
    return joined_along(parts, dim)


def side_by_side(arrays, axis, dim, along):
    both = jnp.concatenate(arrays, axis=along)
    filled, at, gathered = (lax.all_gather(both, axis, axis=dim, tiled=True), 0, [])
    for a in arrays:
        gathered.append(lax.slice_in_dim(filled, at, at + a.shape[along], axis=along))
        at += a.shape[along]
    return tuple(gathered)


def collected_together(array, axis):
    leaves = jax.tree.leaves(array)
    sequence = sorted(range(len(leaves)), key=lambda k: -leaves[k].size)
    width = (1, *leaves[sequence[0]].shape)[-1]
    lines = [
        jnp.pad(leaves[k].reshape(-1), (0, -leaves[k].size % width)).reshape(-1, width)
        for k in sequence
    ]
    both, at, found = (lax.all_gather(jnp.concatenate(lines), axis), 0, {})
    for k, line in zip(sequence, lines):
        section = both[:, at : at + len(line)].reshape(len(both), -1)
        found[k] = section[:, : leaves[k].size].reshape(-1, *leaves[k].shape)
        at += len(line)
    numbers = iter(range(len(leaves)))
    return jax.tree.map(lambda _: found[next(numbers)], array)


def combined_by_axis(array, axes, combine):
    for axis in axes:
        pieces = collected_together(array, axis)
        array = jax.tree.map(lambda part: part[0], pieces)
        for k in range(1, lax.axis_size(axis)):
            array = combine(array, jax.tree.map(lambda part: part[k], pieces))
    return array


def cut_along(array, dim, size):
    shape = array.shape
    parts = array.reshape(*shape[:dim], size, shape[dim] // size, *shape[dim + 1 :])
    return jnp.moveaxis(parts, dim, 0)


def sum_at_owner(array, axis, dim):
    parts = cut_along(array, dim, lax.axis_size(axis))
    arrived = lax.all_to_all(parts, axis, split_axis=0, concat_axis=0, tiled=True)
    return arrived.sum(axis=0)


def over_pieces(array, axis):
    return lax.all_gather(array, axis).sum(0)


def over_copies(array, axis):
    return sent_to_all(array, axis).sum(axis=0)


def in_one(arrays, axis):
    vector, at, gathered = (jnp.concatenate([a.reshape(-1) for a in arrays]), 0, [])
    so_far = over_copies(vector, axis)
    for a in arrays:
        gathered.append(so_far[at : at + a.size].reshape(a.shape))
        at += a.size
    return tuple(gathered)


def summed_rows(array, axes, dim):
    for axis in axes:
        array = lax.psum_scatter(array, axis, scatter_dimension=dim, tiled=True)
    return array


def rope_angles(lengths):
    frequencies = rope_base ** (-(jnp.arange(HD // 2, dtype=jnp.float32) * 2.0) / HD)
    return lengths.astype(jnp.float32)[:, None] * frequencies[None, :]


def rotate(vectors, angles):
    middle_index = vectors.shape[-1] // 2
    cosine = jnp.cos(angles)[:, None, :]
    sine = jnp.sin(angles)[:, None, :]
    lower = vectors[..., :middle_index]
    upper = vectors[..., middle_index:]
    return jnp.concatenate([lower * cosine - upper * sine, upper * cosine + lower * sine], axis=-1)


def spread_rows(shard):
    across = whole_of(shard, TP, (0, 1), 2)
    return gathered_copies(across, "sub", 1)


def half_rows_of(shard):
    return whole_of(shard, TP, (0, 1), 2)


def join_partials(earlier, later):
    earlier_max, earlier_sum, earlier_out = earlier
    later_max, later_sum, later_out = later
    highest = jnp.maximum(earlier_max, later_max)
    earlier_scale = jnp.exp(earlier_max - highest)
    later_scale = jnp.exp(later_max - highest)
    joined_sum = earlier_sum * earlier_scale + later_sum * later_scale
    joined_out = earlier_out * earlier_scale[..., None] + later_out * later_scale[..., None]
    return (highest, joined_sum, joined_out)


def per_device(
    hidden_in,
    norm_attn,
    w_query,
    w_key,
    w_value,
    w_out,
    norm_ffn,
    w_gate,
    w_up,
    w_down,
    cache_keys,
    cache_values,
    lengths,
):
    seq_count = hidden_in.shape[0]
    shard_width = hidden_in.shape[2]
    half_width = shard_width * lax.axis_size(TP)
    model_width = half_width * lax.axis_size("sub")
    tp_pos = lax.axis_index(TP)
    sub_pos = lax.axis_index("sub")
    residual = hidden_in.astype(jnp.float32)
    whole_rows = spread_rows(hidden_in).astype(jnp.float32)
    factor = lax.rsqrt(jnp.mean(whole_rows * whole_rows, axis=(1, 2)) + epsilon)
    gain_whole = norm_attn.reshape(whole_rows.shape[1], half_width)
    gathered = (whole_rows * factor[:, None, None] * gain_whole).astype(jnp.bfloat16)
    flattened = gathered.reshape(seq_count, model_width)
    query_part = jnp.dot(
        flattened, w_query.reshape(model_width, -1), preferred_element_type=jnp.float32
    ).astype(jnp.bfloat16)
    key_part = jnp.dot(
        flattened, w_key.reshape(model_width, -1), preferred_element_type=jnp.float32
    ).astype(jnp.bfloat16)
    value_part = jnp.dot(
        flattened, w_value.reshape(model_width, -1), preferred_element_type=jnp.float32
    ).astype(jnp.bfloat16)
    query, key_new, value_new = (
        lax.all_gather(query_part, TP, axis=1, tiled=True),
        *side_by_side((key_part, value_part), TP, 1, 0),
    )
    query_heads = query.shape[1] // HD
    kv_heads = key_new.shape[1] // HD
    group_size = query_heads // kv_heads
    angles = rope_angles(lengths)
    query_rot = rotate(
        query.astype(jnp.float32).reshape(seq_count, query_heads, HD), angles
    ).astype(jnp.bfloat16)
    key_rot = rotate(key_new.astype(jnp.float32).reshape(seq_count, kv_heads, HD), angles).astype(
        jnp.bfloat16
    )
    grouped = query_rot.reshape(seq_count, kv_heads, group_size, HD)
    values_new = value_new.astype(jnp.float32).reshape(seq_count, kv_heads, 1, HD)
    span = cache_keys.shape[1]
    scores = jnp.einsum(
        "bkgd,blkd->bkgl", grouped, cache_keys, preferred_element_type=jnp.float32
    ) / math.sqrt(HD)
    places = tp_pos * span + jnp.arange(span, dtype=jnp.int32)
    live = (places[None, :] < lengths[:, None])[:, None, None, :]
    masked = jnp.where(live, scores, floor_score)
    local_max = jnp.max(masked, axis=-1)
    weights = jnp.where(live, jnp.exp(masked - local_max[..., None]), 0.0)
    local_sum = jnp.sum(weights, axis=-1)
    local_out = jnp.einsum(
        "bkgl,blkd->bkgd",
        weights,
        cache_values.astype(jnp.float32),
        precision=lax.Precision.HIGHEST,
    )
    own_score = jnp.sum(
        grouped.astype(jnp.float32) * key_rot.astype(jnp.float32)[:, :, None, :], axis=-1
    ) / math.sqrt(HD)
    joined_max, joined_sum, joined_out = combined_by_axis(
        (local_max, local_sum, local_out), TP, join_partials
    )
    highest = jnp.maximum(joined_max, own_score)
    kept_scale = jnp.exp(joined_max - highest)
    own_weight = jnp.exp(own_score - highest)
    numerator = joined_out * kept_scale[..., None] + own_weight[..., None] * values_new
    denominator = joined_sum * kept_scale + own_weight
    attended = (numerator / denominator[..., None]).reshape(seq_count, -1).astype(jnp.bfloat16)
    out_part = jnp.dot(
        attended, w_out.reshape(attended.shape[1], -1), preferred_element_type=jnp.float32
    )
    out_part = out_part.reshape(seq_count, -1, shard_width)
    mixed = sum_at_owner(out_part, "sub", 1)
    middle = (residual + mixed).astype(jnp.bfloat16)
    middle_float = middle.astype(jnp.float32)
    raw_half = half_rows_of(middle).astype(jnp.float32)
    partial_squares = jnp.sum(raw_half * raw_half, axis=(1, 2))
    squares_mid = over_pieces(partial_squares, "sub")
    factor_mid = lax.rsqrt(squares_mid / model_width + epsilon)
    gain_half = lax.dynamic_slice_in_dim(norm_ffn, sub_pos * half_width, half_width)
    half_rows = (raw_half * factor_mid[:, None, None] * gain_half).astype(jnp.bfloat16)
    half_flat = half_rows.reshape(seq_count, half_width)
    gate_part = jnp.dot(
        half_flat, w_gate.reshape(half_width, -1), preferred_element_type=jnp.float32
    )
    up_part = jnp.dot(half_flat, w_up.reshape(half_width, -1), preferred_element_type=jnp.float32)
    gate_total, up_total = in_one((gate_part, up_part), "sub")
    hidden = (jax.nn.silu(gate_total) * up_total).astype(jnp.bfloat16)
    down_part = jnp.dot(
        hidden, w_down.reshape(hidden.shape[1], -1), preferred_element_type=jnp.float32
    )
    down_share = summed_rows(down_part, TP, 1)
    return (middle_float + down_share[:, None, :]).astype(jnp.bfloat16)


def solution(mesh):
    split = Mesh(
        mesh.devices.reshape(mesh.shape["grp"], 8, 16, mesh.shape["sub"]),
        ("grp", "tp_0", "tp_1", "sub"),
    )
    return jax.shard_map(
        per_device,
        mesh=split,
        in_specs=(
            P("grp", "sub", TP),
            P(),
            P(None, "sub", TP),
            P(None, "sub", TP),
            P(None, "sub", TP),
            P("sub", None, None, TP),
            P(),
            P("sub", None, TP),
            P("sub", None, TP),
            P(TP, "sub", None),
            P("grp", TP, "sub", None),
            P("grp", TP, "sub", None),
            P("grp"),
        ),
        out_specs=P("grp", "sub", TP),
        check_vma=False,
    )
```

profile of v0, /device:TPU:66, one launch (start us, length us, event | category | flops | bytes accessed | tf_op | source)
XLA Modules:
  0.0 595.9 jit_solution(17651004225491951101)
XLA Ops:
  6.6 62.3 %all-gather = bf16[128,1,32]{2,0,1:T(8,128)(2,1)S(1)} all-gather(bf16[16,1,32]{2,0,1:T(8,128)(2,1)} %param.13), channel_id=2, replica_groups=mesh['grp'=2,'tp_0'=8,'tp_1'=16,'sub'=2] {'tp_0'}, dimensions={0}, use_global_device_ids=true | all-gather | bytes 9216 | tf_op jit(solution)/shard_map/all_gather | solution.py:24
  68.8 34.6 %all_gather.37 = bf16[128,16,1,32]{3,1,2,0:T(8,128)(2,1)S(1)} all-gather(bf16[8,16,1,32]{3,1,2,0:T(8,128)(2,1)S(1)} %bitcast.547), channel_id=1, replica_groups=mesh['grp'=2,'tp_0'=8,'tp_1'=16,'sub'=2] {'tp_1'}, dimensions={0}, use_global_device_ids=true | all-gather | bytes 139264 | tf_op jit(solution)/shard_map/all_gather | solution.py:24
  104.1 0.7 broadcast_in_dim.30
  104.9 3.5 all-to-all-start
  108.6 1.3 all-to-all-done
  110.9 87.2 %all-gather.5 = bf16[128,32,16]{1,2,0:T(8,128)(2,1)S(1)} all-gather(bf16[1,32,16]{1,2,0:T(8,128)(2,1)S(1)} %fusion.1), channel_id=1, replica_groups=mesh['grp'=2,'tp_0'=8,'tp_1'=16,'sub'=2] {'tp_0','tp_1'}, dimensions={0}, use_global_device_ids=true | all-gather | bytes 132096 | tf_op jit(solution)/shard_map/all_gather | solution.py:186
  201.9 39.4 %all-gather.10.cloned.1.call-done = f32[4160,128]{1,0:T(8,128)} async-done(((f32[520,128]{1,0:T(8,128)}), f32[4160,128]{1,0:T(8,128)}) %all-gather.10.cloned.1.call-update) | async-done | bytes 2129936 | tf_op jit(solution)/shard_map/all_gather | solution.py:62
  241.3 0.8 fusion.56
  244.9 2.5 fusion.16
  247.4 0.7 pad_maximum_fusion.1
  248.9 89.8 %all-gather.6 = bf16[128,4,32]{2,1,0:T(4,128)(2,1)S(1)} all-gather(bf16[1,4,32]{2,1,0:T(4,128)(2,1)S(1)} %maximum_bitcast_fusion), channel_id=1, replica_groups=mesh['grp'=2,'tp_0'=8,'tp_1'=16,'sub'=2] {'tp_0','tp_1'}, dimensions={0}, use_global_device_ids=true | all-gather | bytes 33024 | tf_op jit(solution)/shard_map/all_gather | solution.py:47
  339.5 1.3 dynamic-slice
  341.6 0.9 multiply_reduce_fusion
  342.5 1.4 fusion.109
  343.9 1.5 fusion.108
  345.4 3.5 fusion.110
  348.8 1.4 squeeze.268
  350.2 1.4 squeeze.288
  351.6 1.4 squeeze.286
  353.0 1.4 squeeze.284
  354.3 1.4 squeeze.282
  355.7 1.4 squeeze.280
  357.1 1.4 squeeze.278
  358.5 1.4 squeeze.276
  359.9 1.4 squeeze.274
  361.2 1.4 squeeze.272
  362.6 1.4 squeeze.270
  364.0 1.3 squeeze.266
  365.3 1.4 squeeze.265
  366.7 1.4 squeeze.294
  368.1 1.4 squeeze.292
  369.5 1.4 squeeze.290
  370.9 1.4 squeeze.311
  372.2 1.4 squeeze.310
  373.6 1.4 squeeze.309
  375.0 1.4 squeeze.308
  376.4 1.4 squeeze.307
  377.7 1.4 squeeze.306
  379.1 1.4 squeeze.305
  380.5 1.4 squeeze.304
  381.9 1.4 squeeze.303
  383.3 1.4 squeeze.302
  384.7 1.4 squeeze.301
  386.0 1.4 squeeze.300
  387.4 1.4 squeeze.299
  388.8 1.4 squeeze.298
  390.2 1.4 squeeze.297
  391.6 1.4 squeeze.296
  393.0 1.1 maximum_maximum_fusion
  394.1 1.7 multiply_add_fusion
  395.9 3.3 divide_convert_fusion
  399.2 1.0 reshape.2406
  400.2 1.5 fusion.113
  401.7 3.7 all_to_all.16
  407.4 24.7 %all-gather.3 = bf16[128,1,32]{2,0,1:T(8,128)(2,1)S(1)} all-gather(bf16[16,1,32]{2,0,1:T(8,128)(2,1)S(1)} %fusion.51), channel_id=5, replica_groups=mesh['grp'=2,'tp_0'=8,'tp_1'=16,'sub'=2] {'tp_0'}, dimensions={0}, use_global_device_ids=true | all-gather | bytes 9216 | tf_op jit(solution)/shard_map/all_gather | solution.py:24
  432.2 30.3 %all_gather.45 = bf16[128,16,1,32]{3,1,2,0:T(8,128)(2,1)S(1)} all-gather(bf16[8,16,1,32]{3,1,2,0:T(8,128)(2,1)S(1)} %bitcast.548), channel_id=1, replica_groups=mesh['grp'=2,'tp_0'=8,'tp_1'=16,'sub'=2] {'tp_1'}, dimensions={0}, use_global_device_ids=true | all-gather | bytes 139264 | tf_op jit(solution)/shard_map/all_gather | solution.py:24
  463.1 2.5 all-reduce
  467.4 1.6 fusion.7
  469.2 3.8 all_to_all.17
  473.1 1.0 fusion.3
  474.2 39.7 %reduce-scatter.5.cloned.1.call-done = f32[16,512]{1,0:T(8,128)} async-done(((f32[16,4096]{1,0:T(8,128)}), f32[16,512]{1,0:T(8,128)}) %reduce-scatter.5.cloned.1.call-update) | async-done | bytes 32784 | tf_op jit(solution)/shard_map/reduce_scatter | solution.py:111
  514.0 1.6 copy.106
  515.6 72.4 %reduce-scatter.7.cloned.1.call-done = f32[32,16]{1,0:T(8,128)} async-done(((f32[512,16]{1,0:T(8,128)}), f32[32,16]{1,0:T(8,128)}) %reduce-scatter.7.cloned.1.call-update) | async-done | bytes 2064
  588.0 0.8 copy.107
  (109 shorter events, 15.7 us)
Async XLA Ops:
  6.5 466.6 %copy-start = (bf16[112,1,4096]{2,0,1:T(8,128)(2,1)S(1)}, bf16[112,1,4096]{2,0,1:T(8,128)(2,1)}, u32[]{:S(2)}) copy-start(bf16[112,1,4096]{2,0,1:T(8,128)(2,1)} %param.22) | copy-start | bytes 2752516
  68.8 39.6 %copy-start.14 = (s32[16]{0:T(128)S(1)}, s32[16]{0:T(128)}, u32[]{:S(2)}) copy-start(s32[16]{0:T(128)} %param.25) | copy-start | bytes 196
  68.8 39.7 %copy-start.12 = (f32[8192]{0:T(1024)S(1)}, f32[8192]{0:T(1024)}, u32[]{:S(2)}) copy-start(f32[8192]{0:T(1024)} %param.14) | copy-start | bytes 98308
  103.4 7.2 %copy-start.8 = (bf16[8192,1,32]{0,2,1:T(8,128)(2,1)S(1)}, bf16[8192,1,32]{0,2,1:T(8,128)(2,1)}, u32[]{:S(2)}) copy-start(bf16[8192,1,32]{0,2,1:T(8,128)(2,1)} %param.15) | copy-start | bytes 1572868
  104.9 5.0 all-to-all-start
  108.3 132.9 %all-gather.10.cloned.1.call-start = ((), (), s32[]{:S(2)}) async-start(), calls=%async_computation.6 | async-start | bytes 2396160 | tf_op jit(solution)/shard_map/all_gather | solution.py:62
  198.1 1.6 copy-start.10
  198.9 1.5 copy-start.11
  200.9 47.5 %copy-start.15 = (bf16[8192,1,4]{0,2,1:T(4,128)(2,1)S(1)}, bf16[8192,1,4]{0,2,1:T(4,128)(2,1)}, u32[]{:S(2)}) copy-start(bf16[8192,1,4]{0,2,1:T(4,128)(2,1)} %param.17) | copy-start | bytes 196612
  201.0 47.6 %copy-start.16 = (bf16[8192,1,4]{0,2,1:T(4,128)(2,1)S(1)}, bf16[8192,1,4]{0,2,1:T(4,128)(2,1)}, u32[]{:S(2)}) copy-start(bf16[8192,1,4]{0,2,1:T(4,128)(2,1)} %param.16) | copy-start | bytes 196612
  201.8 140.7 %all-gather.12.cloned.1.call-start = ((), (), s32[]{:S(2)}) async-start(), calls=%async_computation.7 | async-start | bytes 4526080 | tf_op jit(solution)/shard_map/all_gather | solution.py:62
  244.9 96.5 %copy-start.13 = (f32[8192]{0:T(1024)S(1)}, f32[8192]{0:T(1024)}, u32[]{:S(2)}) copy-start(f32[8192]{0:T(1024)} %param.19) | copy-start | bytes 98308
  248.2 265.8 %reduce-scatter.5.cloned.1.call-start = ((), (), s32[]{:S(2)}) async-start(), calls=%async_computation.5 | async-start | bytes 294912 | tf_op jit(solution)/shard_map/reduce_scatter | solution.py:111
  392.9 2.9 copy-start.1
  392.9 2.9 copy-start.2
  392.9 2.9 copy-start.3
  392.9 3.0 copy-start.4
  392.9 3.0 copy-start.5
  393.0 3.0 copy-start.6
  393.0 3.0 copy-start.9
  465.8 1.2 copy-start.7
  474.1 113.9 %reduce-scatter.7.cloned.1.call-start = ((), (), s32[]{:S(2)}) async-start(), calls=%async_computation.8 | async-start | bytes 278528
Sparse Core Ops, SparseCore 0:
  201.9 39.2 all-gather.9
  248.3 79.5 all-gather.11
  474.3 39.6 reduce-scatter.4
  516.6 71.3 reduce-scatter.6
where the time goes:
time: 598 us; the launch traced here: 596 us
  blocking collectives  339 us (57%)
  waiting for transfers between devices  153 us (26%)
  local copies, waits for them, and re-layouts  61.8 us (10%)
  other arithmetic  18.1 us (3%)
  between operations  14.3 us (2%)
    all_gather x4, blocking collectives, gather_in_order(): parts = lax.all_gather(parts, axes[k], axis=0, tiled=True)  152 us
    all_gather x1, blocking collectives, side_by_side(): lax.all_gather(both, axis, axis=dim, tiled=True)  89.8 us
    all_gather x1, blocking collectives, per_device(): lax.all_gather(query_part, TP, axis=1, tiled=True)  87.2 us
    unnamed x5, waiting for transfers between devices  72.6 us
    squeeze x30, local copies, waits for them, and re-layouts, combined_by_axis(): array = combine(array, jax.tree.map(lambda part: part[k], pieces))  41.3 us
    reduce_scatter x1, waiting for transfers between devices, summed_rows(): array = lax.psum_scatter(array, axis, scatter_dimension=dim, tiled=True)  39.7 us
    all_gather x2, waiting for transfers between devices, collected_together(): both, at, found = (lax.all_gather(jnp.concatenate(lines), axis), 0, {})  39.4 us
  transfers between devices with their start and end apart: 5, of which 4 were waited for; matrix products, arithmetic and copies ran while one was open for 1% of the time, Pallas kernels for 0%

commit v1 on v0

--- a/solution.py
+++ b/solution.py
@@ -183,7 +183,9 @@
         flattened, w_value.reshape(model_width, -1), preferred_element_type=jnp.float32
     ).astype(jnp.bfloat16)
     query, key_new, value_new = (
-        lax.all_gather(query_part, TP, axis=1, tiled=True),
+        jnp.concatenate(
+            lax.all_to_all(jnp.stack([query_part] * lax.axis_size(TP)), TP, 0, 0), axis=1
+        ),
         *side_by_side((key_part, value_part), TP, 1, 0),
     )
     query_heads = query.shape[1] // HD

time: 598 us -> 537 us (0.90)
  blocking collectives: 339 us -> 252 us
  waiting for transfers between devices: 153 us -> 167 us
  starting transfers between devices: 3.91 us -> 14.9 us
    all_gather x1 -> x0, blocking collectives: 87.2 us -> none  [per_device(): lax.all_gather(query_part, TP, axis=1, tiled=True)]
    all_to_all x0 -> x1, waiting for transfers between devices: none -> 17.4 us  [per_device(): lax.all_to_all(jnp.stack([query_part] * lax.axis_size(TP)), TP, 0, 0)]
    all_to_all x0 -> x1, starting transfers between devices: none -> 11.1 us  [per_device(): lax.all_to_all(jnp.stack([query_part] * lax.axis_size(TP)), TP, 0, 0)]
  transfers between devices with their start and end apart: 5 -> 6, of which waited for: 4 -> 5; matrix products, arithmetic and copies ran while one was open for 1% -> 1% of each run, Pallas kernels for 0% -> 0%
where the time goes in v1:
time: 537 us; the launch traced here: 535 us
  blocking collectives  252 us (47%)
  waiting for transfers between devices  167 us (31%)
  local copies, waits for them, and re-layouts  62.6 us (12%)
  other arithmetic  18.2 us (3%)
  starting transfers between devices  14.9 us (3%)
  between operations  14.4 us (3%)
  matrix products  5.95 us (1%)
    all_gather x4, blocking collectives, gather_in_order(): parts = lax.all_gather(parts, axes[k], axis=0, tiled=True)  152 us
    all_gather x1, blocking collectives, side_by_side(): lax.all_gather(both, axis, axis=dim, tiled=True)  90.1 us
    unnamed x5, waiting for transfers between devices  72.4 us
    squeeze x30, local copies, waits for them, and re-layouts, combined_by_axis(): array = combine(array, jax.tree.map(lambda part: part[k], pieces))  41.3 us
    reduce_scatter x1, waiting for transfers between devices, summed_rows(): array = lax.psum_scatter(array, axis, scatter_dimension=dim, tiled=True)  39.7 us
    all_gather x2, waiting for transfers between devices, collected_together(): both, at, found = (lax.all_gather(jnp.concatenate(lines), axis), 0, {})  36.3 us
    all_to_all x1, waiting for transfers between devices, per_device(): lax.all_to_all(jnp.stack([query_part] * lax.axis_size(TP)), TP, 0, 0)  17.4 us
    all_to_all x1, starting transfers between devices, per_device(): lax.all_to_all(jnp.stack([query_part] * lax.axis_size(TP)), TP, 0, 0)  11.1 us
  transfers between devices with their start and end apart: 6, of which 5 were waited for; matrix products, arithmetic and copies ran while one was open for 1% of the time, Pallas kernels for 0%

profile of v1, /device:TPU:66, one launch (start us, length us, event | category | flops | bytes accessed | tf_op | source)
XLA Modules:
  0.0 535.0 jit_solution(322187194634552637)
XLA Ops:
  6.6 62.3 %all-gather = bf16[128,1,32]{2,0,1:T(8,128)(2,1)S(1)} all-gather(bf16[16,1,32]{2,0,1:T(8,128)(2,1)} %param.13), channel_id=2, replica_groups=mesh['grp'=2,'tp_0'=8,'tp_1'=16,'sub'=2] {'tp_0'}, dimensions={0}, use_global_device_ids=true | all-gather | bytes 9216 | tf_op jit(solution)/shard_map/all_gather | solution.py:24
  68.8 34.4 %all_gather.34 = bf16[128,16,1,32]{3,1,2,0:T(8,128)(2,1)S(1)} all-gather(bf16[8,16,1,32]{3,1,2,0:T(8,128)(2,1)S(1)} %bitcast.538), channel_id=1, replica_groups=mesh['grp'=2,'tp_0'=8,'tp_1'=16,'sub'=2] {'tp_1'}, dimensions={0}, use_global_device_ids=true | all-gather | bytes 139264 | tf_op jit(solution)/shard_map/all_gather | solution.py:24
  104.7 3.5 all-to-all-start
  108.2 1.5 all-to-all-done
  110.8 1.0 reshape.2405
  111.9 11.1 %all-to-all-start.1 = ((bf16[128,2,256]{2,1,0:T(2,128)(2,1)}), bf16[128,2,256]{2,1,0:T(2,128)(2,1)S(1)}, u32[]{:S(2)}, u32[]{:S(2)}) async-start(bf16[128,2,256]{2,1,0:T(2,128)(2,1)} %reshape.2405), calls=%async_computation.1 | async-start | bytes 262144 | tf_op jit(solution)/shard_map/all_to_all | solution.py:187
  123.3 17.4 %all-to-all-done.1 = bf16[128,2,256]{2,1,0:T(2,128)(2,1)S(1)} async-done(((bf16[128,2,256]{2,1,0:T(2,128)(2,1)}), bf16[128,2,256]{2,1,0:T(2,128)(2,1)S(1)}, u32[]{:S(2)}, u32[]{:S(2)}) %all-to-all-start.1) | async-done | bytes 131104 | tf_op jit(solution)/shard_map/all_to_all | solution.py:187
  144.2 36.3 %all-gather.9.cloned.1.call-done = f32[4160,128]{1,0:T(8,128)} async-done(((f32[520,128]{1,0:T(8,128)}), f32[4160,128]{1,0:T(8,128)}) %all-gather.9.cloned.1.call-update) | async-done | bytes 2129936 | tf_op jit(solution)/shard_map/all_gather | solution.py:62
  180.5 0.8 fusion.55
  184.1 2.5 fusion.15
  188.0 90.1 %all-gather.5 = bf16[128,4,32]{2,1,0:T(4,128)(2,1)S(1)} all-gather(bf16[1,4,32]{2,1,0:T(4,128)(2,1)S(1)} %maximum_bitcast_fusion), channel_id=1, replica_groups=mesh['grp'=2,'tp_0'=8,'tp_1'=16,'sub'=2] {'tp_0','tp_1'}, dimensions={0}, use_global_device_ids=true | all-gather | bytes 33024 | tf_op jit(solution)/shard_map/all_gather | solution.py:47
  278.8 1.3 dynamic-slice
  280.9 0.9 multiply_reduce_fusion
  281.8 1.4 fusion.108
  283.2 1.5 fusion.107
  284.7 3.5 fusion.109
  288.2 1.4 squeeze.268
  289.6 1.3 squeeze.288
  290.9 1.4 squeeze.286
  292.3 1.4 squeeze.284
  293.7 1.4 squeeze.282
  295.0 1.4 squeeze.280
  296.4 1.4 squeeze.278
  297.8 1.4 squeeze.276
  299.2 1.4 squeeze.274
  300.5 1.4 squeeze.272
  301.9 1.4 squeeze.270
  303.3 1.4 squeeze.266
  304.7 1.4 squeeze.265
  306.1 1.4 squeeze.294
  307.5 1.3 squeeze.292
  308.8 1.4 squeeze.290
  310.2 1.4 squeeze.311
  311.5 1.4 squeeze.310
  312.9 1.4 squeeze.309
  314.3 1.4 squeeze.308
  315.7 1.4 squeeze.307
  317.0 1.4 squeeze.306
  318.4 1.4 squeeze.305
  319.8 1.4 squeeze.304
  321.2 1.4 squeeze.303
  322.6 1.4 squeeze.302
  324.0 1.4 squeeze.301
  325.3 1.4 squeeze.300
  326.7 1.4 squeeze.299
  328.1 1.4 squeeze.298
  329.5 1.4 squeeze.297
  330.9 1.4 squeeze.296
  332.3 1.1 maximum_maximum_fusion
  333.4 1.7 multiply_add_fusion
  335.3 3.3 divide_convert_fusion
  338.5 1.0 reshape.2400
  339.5 1.5 fusion.112
  341.1 3.7 all_to_all.21
  346.8 24.6 %all-gather.3 = bf16[128,1,32]{2,0,1:T(8,128)(2,1)S(1)} all-gather(bf16[16,1,32]{2,0,1:T(8,128)(2,1)S(1)} %fusion.50), channel_id=5, replica_groups=mesh['grp'=2,'tp_0'=8,'tp_1'=16,'sub'=2] {'tp_0'}, dimensions={0}, use_global_device_ids=true | all-gather | bytes 9216 | tf_op jit(solution)/shard_map/all_gather | solution.py:24
  371.4 30.3 %all_gather.41 = bf16[128,16,1,32]{3,1,2,0:T(8,128)(2,1)S(1)} all-gather(bf16[8,16,1,32]{3,1,2,0:T(8,128)(2,1)S(1)} %bitcast.539), channel_id=1, replica_groups=mesh['grp'=2,'tp_0'=8,'tp_1'=16,'sub'=2] {'tp_1'}, dimensions={0}, use_global_device_ids=true | all-gather | bytes 139264 | tf_op jit(solution)/shard_map/all_gather | solution.py:24
  402.4 2.5 all-reduce
  406.6 1.6 fusion.6
  408.4 3.8 all_to_all.22
  412.4 0.9 fusion.2
  413.5 39.7 %reduce-scatter.5.cloned.1.call-done = f32[16,512]{1,0:T(8,128)} async-done(((f32[16,4096]{1,0:T(8,128)}), f32[16,512]{1,0:T(8,128)}) %reduce-scatter.5.cloned.1.call-update) | async-done | bytes 32784 | tf_op jit(solution)/shard_map/reduce_scatter | solution.py:111
  453.1 1.6 copy.102
  454.8 72.2 %reduce-scatter.7.cloned.1.call-done = f32[32,16]{1,0:T(8,128)} async-done(((f32[512,16]{1,0:T(8,128)}), f32[32,16]{1,0:T(8,128)}) %reduce-scatter.7.cloned.1.call-update) | async-done | bytes 2064
  527.0 0.8 copy.103
  (112 shorter events, 16.9 us)
Async XLA Ops:
  6.5 405.9 %copy-start = (bf16[112,1,4096]{2,0,1:T(8,128)(2,1)S(1)}, bf16[112,1,4096]{2,0,1:T(8,128)(2,1)}, u32[]{:S(2)}) copy-start(bf16[112,1,4096]{2,0,1:T(8,128)(2,1)} %param.22) | copy-start | bytes 2752516
  6.6 101.6 %copy-start.12 = (f32[8192]{0:T(1024)S(1)}, f32[8192]{0:T(1024)}, u32[]{:S(2)}) copy-start(f32[8192]{0:T(1024)} %param.14) | copy-start | bytes 98308
  103.3 7.2 %copy-start.8 = (bf16[8192,1,32]{0,2,1:T(8,128)(2,1)S(1)}, bf16[8192,1,32]{0,2,1:T(8,128)(2,1)}, u32[]{:S(2)}) copy-start(bf16[8192,1,32]{0,2,1:T(8,128)(2,1)} %param.15) | copy-start | bytes 1572868
  104.7 5.0 all-to-all-start
  108.2 14.9 %copy-start.14 = (s32[16]{0:T(128)S(1)}, s32[16]{0:T(128)}, u32[]{:S(2)}) copy-start(s32[16]{0:T(128)} %param.25) | copy-start | bytes 196
  111.9 28.9 %all-to-all-start.1 = ((bf16[128,2,256]{2,1,0:T(2,128)(2,1)}), bf16[128,2,256]{2,1,0:T(2,128)(2,1)S(1)}, u32[]{:S(2)}, u32[]{:S(2)}) async-start(bf16[128,2,256]{2,1,0:T(2,128)(2,1)} %reshape.2405), calls=%async_computation.1 | async-start | bytes 262144 | tf_op jit(solution)/shard_map/all_to_all | solution.py:187
  123.0 57.5 %all-gather.9.cloned.1.call-start = ((), (), s32[]{:S(2)}) async-start(), calls=%async_computation.7 | async-start | bytes 2396160 | tf_op jit(solution)/shard_map/all_gather | solution.py:62
  141.1 0.9 copy-start.10
  141.1 1.5 copy-start.11
  143.2 44.3 %copy-start.15 = (bf16[8192,1,4]{0,2,1:T(4,128)(2,1)S(1)}, bf16[8192,1,4]{0,2,1:T(4,128)(2,1)}, u32[]{:S(2)}) copy-start(bf16[8192,1,4]{0,2,1:T(4,128)(2,1)} %param.17) | copy-start | bytes 196612
  143.3 44.4 %copy-start.16 = (bf16[8192,1,4]{0,2,1:T(4,128)(2,1)S(1)}, bf16[8192,1,4]{0,2,1:T(4,128)(2,1)}, u32[]{:S(2)}) copy-start(bf16[8192,1,4]{0,2,1:T(4,128)(2,1)} %param.16) | copy-start | bytes 196612
  144.1 137.7 %all-gather.11.cloned.1.call-start = ((), (), s32[]{:S(2)}) async-start(), calls=%async_computation.8 | async-start | bytes 4526080 | tf_op jit(solution)/shard_map/all_gather | solution.py:62
  184.1 96.6 %copy-start.13 = (f32[8192]{0:T(1024)S(1)}, f32[8192]{0:T(1024)}, u32[]{:S(2)}) copy-start(f32[8192]{0:T(1024)} %param.19) | copy-start | bytes 98308
  187.4 265.8 %reduce-scatter.5.cloned.1.call-start = ((), (), s32[]{:S(2)}) async-start(), calls=%async_computation.6 | async-start | bytes 294912 | tf_op jit(solution)/shard_map/reduce_scatter | solution.py:111
  332.3 2.9 copy-start.1
  332.3 2.9 copy-start.2
  332.3 2.9 copy-start.3
  332.3 3.0 copy-start.4
  332.3 3.0 copy-start.5
  332.3 3.0 copy-start.6
  332.3 3.0 copy-start.9
  405.1 1.2 copy-start.7
  413.4 113.6 %reduce-scatter.7.cloned.1.call-start = ((), (), s32[]{:S(2)}) async-start(), calls=%async_computation.9 | async-start | bytes 278528
Sparse Core Ops, SparseCore 0:
  144.2 36.1 all-gather.8
  187.5 79.5 all-gather.10
  413.5 39.5 reduce-scatter.4
  455.8 71.1 reduce-scatter.6
